TPU v7x, 128 devices: a whole 4x4x4 slice. The times are simulated.
128 devices in a mesh: samp: 16 (over z, x), feat: 8 (over y, core).
Axes of the slice: x: 4, y: 4, z: 4, core: 2. Of those that a mesh axis runs over, the one named last changes fastest.
Arguments:
- features: bfloat16 [262144, 2048], P('samp', 'feat'), may hold values from -40 to 40
- labels: int32 [262144], P('samp'), may hold values from 0 to 9
- weights: float32 [10, 2048], P(None, 'feat'), may hold values from -6 to 6
- sketch_basis: float32 [10, 2048, 512], P(None, 'feat'), may hold values from -0.0390625 to 0.0390625
- sketch_values: float32 [512], replicated, may hold values from 0.05 to 2
Outputs:
- newton_step: float32 [10, 2048], P(None, 'feat')
All inputs are finite; a program needn't handle non-finite values.
Results may differ from a plain program's by a relative error of at most 0.001.
The roundings to bfloat16 on the way count: a program that leaves them out, or rounds other values in their place, can miss the bound.
Values may be sent and summed in bfloat16 or wider, within the bound.
A program may use at most 128 MiB of HBM per device.

v0:
```python
import math
import jax
import jax.numpy as jnp
from jax import lax
from jax.sharding import PartitionSpec as P

F = 2048
ITERS = 3
ridge = 0.05
contract_last = (((1,), (1,)), ((), ()))
contract_first = (((0,), (0,)), ((), ()))


def copy_for_each(shard, axis):
    devices = lax.axis_size(axis)
    return lax.all_to_all(
        jnp.broadcast_to(shard[None], (devices, *shard.shape)), axis, 0, 0, tiled=True
    )


def of_everyone(shard, axis):
    everything = copy_for_each(shard, axis)
    return jnp.sum(everything, axis=0)


def in_blocks(shard, dim, devices):
    before, after = (shard.shape[:dim], shard.shape[dim + 1 :])
    return jnp.moveaxis(shard.reshape(*before, devices, -1, *after), dim, 0)


def summed_on_arrival(shard, axis, dim):
    devices = lax.axis_size(axis)
    pieces = lax.all_to_all(in_blocks(shard, dim, devices), axis, 0, 0, tiled=True)
    return jnp.sum(pieces, axis=0)


def column_softmax(scores):
    column_max = jnp.max(scores, axis=0, keepdims=True)
    shifted_exp = jnp.exp(scores - column_max)
    return shifted_exp / jnp.sum(shifted_exp, axis=0, keepdims=True)


def total_one(amount):
    return of_everyone(amount, "feat")


def on_device(features, labels, weights, sketch_basis, sketch_values):
    classes, local_cols = weights.shape
    local_rows = features.shape[0]
    sketch_rank = sketch_basis.shape[2]
    samp_count = lax.axis_size("samp")
    feat_count = lax.axis_size("feat")
    total_rows = local_rows * samp_count
    row_features = lax.all_to_all(features, "feat", split_axis=0, concat_axis=1, tiled=True)
    share_rows = local_rows // feat_count
    row_start = lax.axis_index("feat") * share_rows
    own_labels = lax.dynamic_slice_in_dim(labels, row_start, share_rows, 0)
    onehot = (own_labels[None, :] == jnp.arange(classes, dtype=jnp.int32)[:, None]).astype(
        jnp.float32
    )

    def class_logits(rounded):
        partial_logits = lax.dot_general(
            rounded, row_features, contract_last, preferred_element_type=jnp.float32
        )
        return partial_logits

    def feature_sums(coeffs):
        coeffs_b = coeffs.astype(jnp.bfloat16)
        whole_cols = jnp.dot(coeffs_b, row_features, preferred_element_type=jnp.float32)
        partial_cols = summed_on_arrival(whole_cols, "feat", 1)
        return of_everyone(partial_cols, "samp")

    weights_b = weights.astype(jnp.bfloat16)
    weights_b = lax.all_gather(weights_b, "feat", axis=1, tiled=True)
    probabilities = column_softmax(class_logits(weights_b) / math.sqrt(F))
    gradient = feature_sums(probabilities - onehot) * (math.sqrt(F) / total_rows) + ridge * weights
    flat_local = sketch_basis.reshape(classes * local_cols, sketch_rank)
    local_gram = lax.dot_general(
        flat_local, flat_local, contract_first, precision=lax.Precision.HIGHEST
    )
    gram_matrix = lax.psum(local_gram, "feat")
    factor = jnp.linalg.cholesky(gram_matrix)
    coefficients = (jnp.min(sketch_values) + ridge) / (sketch_values + ridge) - 1.0
    basis_own = sketch_basis.reshape(classes * local_cols, sketch_rank)

    def precondition(residue):
        local_proj = jnp.dot(residue.reshape(-1), basis_own, precision=lax.Precision.HIGHEST)
        projection = total_one(local_proj)
        inner_coords = jax.scipy.linalg.solve_triangular(factor, projection, lower=True)
        weighted_coords = coefficients * inner_coords
        outer_coords = jax.scipy.linalg.solve_triangular(
            factor, weighted_coords, lower=True, trans=1
        )
        scaled_res = residue + jnp.dot(
            basis_own, outer_coords, precision=lax.Precision.HIGHEST
        ).reshape(residue.shape)
        return (scaled_res, total_one(jnp.sum(residue * scaled_res)))

    residue = -gradient
    newton_part = jnp.zeros_like(residue)
    scaled_res, res_dot = precondition(residue)
    direction = scaled_res
    for iteration in range(ITERS):
        hessian_rounded = direction.astype(jnp.bfloat16)
        gathered = hessian_rounded
        gathered = lax.all_gather(gathered, "feat", axis=1, tiled=True)
        image_vals = class_logits(gathered)
        weighted = probabilities * image_vals
        curvature = weighted - probabilities * jnp.sum(weighted, axis=0, keepdims=True)
        hess_image = feature_sums(curvature) / total_rows + ridge * direction
        step_size = res_dot / total_one(jnp.sum(direction * hess_image))
        newton_part = newton_part + step_size * direction
        if iteration + 1 < ITERS:
            residue = residue - step_size * hess_image
            scaled_res, new_dot = precondition(residue)
            direction = scaled_res + new_dot / res_dot * direction
            res_dot = new_dot
    return newton_part


def solution(mesh):
    in_specs = (P("samp", "feat"), P("samp"), P(None, "feat"), P(None, "feat", None), P())
    out_specs = P(None, "feat")
    return jax.shard_map(
        on_device, mesh=mesh, in_specs=in_specs, out_specs=out_specs, check_vma=False
    )
```

profile of v0, /device:TPU:1, one launch (start us, length us, event | category | flops | bytes accessed | tf_op | source)
XLA Modules:
  0.0 569.8 jit_solution(3799169834706363901)
XLA Ops:
  6.5 6.3 %all-to-all-start = ((bf16[8,2048,256]{2,1,0:T(8,128)(2,1)}), bf16[8,2048,256]{2,1,0:T(8,128)(2,1)}, u32[]{:S(2)}, u32[]{:S(2)}) async-start(bf16[8,2048,256]{2,1,0:T(8,128)(2,1)} %bitcast.495), calls=%async_computation | async-start | bytes 16777216 | tf_op jit(solution)/shard_map/all_to_all | solution.py:54
  12.9 12.3 %convolution_bitcast_fusion = f32[512,512]{0,1:T(8,128)} fusion(f32[10,256,512]{2,1,0:T(8,128)} %param.12), kind=kOutput, calls=%fused_computation.14 | convolution fusion | flops 8053063680 | bytes 6291456 | tf_op jit(solution)/shard_map/dot_general | solution.py:79
  26.5 96.5 %all_gather.12 = bf16[10,2048]{1,0:T(8,128)(2,1)S(1)} all-gather(bf16[10,256]{1,0:T(8,128)(2,1)S(1)} %convert_element_type.27), channel_id=1, replica_groups=mesh['samp'=16,'feat'=8] {'feat'}, dimensions={1}, use_global_device_ids=true | all-gather | bytes 46080 | tf_op jit(solution)/shard_map/all_gather | solution.py:75
  123.0 1.6 copy.18
  124.6 1.4 fusion.56
  126.0 11.7 %cholesky.104 = f32[128,128]{1,0:T(8,128)S(1)} custom-call(f32[128,128]{1,0:T(8,128)S(1)} %cholesky.266), custom_call_target="Cholesky" | custom-call | tf_op jit(solution)/shard_map/jit(cholesky)/cholesky | solution.py:83
  137.9 9.8 %custom-call.33 = f32[1,128,128]{1,2,0:T(8,128)S(1)} custom-call(f32[1,128,128]{2,1,0:T(8,128)S(1)} %get-tuple-element.78), custom_call_target="InvertDiagBlocksLowerTriangular" | custom-call | tf_op jit(solution)/shard_map/jit(cholesky)/cholesky | solution.py:83
  148.4 11.7 %cholesky.217 = f32[128,128]{1,0:T(8,128)S(1)} custom-call(f32[128,128]{1,0:T(8,128)S(1)} %cholesky.270), custom_call_target="Cholesky" | custom-call | tf_op jit(solution)/shard_map/jit(cholesky)/cholesky | solution.py:83
  160.1 10.0 %custom-call.34 = f32[1,128,128]{1,2,0:T(8,128)S(1)} custom-call(f32[1,128,128]{2,1,0:T(8,128)S(1)} %get-tuple-element.75), custom_call_target="InvertDiagBlocksLowerTriangular" | custom-call | tf_op jit(solution)/shard_map/jit(cholesky)/cholesky | solution.py:83
  170.8 11.7 %cholesky.238 = f32[128,128]{1,0:T(8,128)S(1)} custom-call(f32[128,128]{1,0:T(8,128)S(1)} %cholesky.275), custom_call_target="Cholesky" | custom-call | tf_op jit(solution)/shard_map/jit(cholesky)/cholesky | solution.py:83
  182.5 9.8 %custom-call.35 = f32[1,128,128]{1,2,0:T(8,128)S(1)} custom-call(f32[1,128,128]{2,1,0:T(8,128)S(1)} %get-tuple-element.72), custom_call_target="InvertDiagBlocksLowerTriangular" | custom-call | tf_op jit(solution)/shard_map/jit(cholesky)/cholesky | solution.py:83
  192.9 11.9 %cholesky.255 = f32[128,128]{1,0:T(8,128)S(1)} custom-call(f32[128,128]{1,0:T(8,128)S(1)} %convolution_subtract_fusion.2), custom_call_target="Cholesky" | custom-call | tf_op jit(solution)/shard_map/jit(cholesky)/cholesky | solution.py:83
  204.8 0.7 compare_reduce_fusion.2
  206.8 0.7 compare_reduce_fusion.1
  208.2 11.6 %copy.14 = bf16[2048,8,256]{0,2,1:T(8,128)(2,1)} copy(bf16[2048,8,256]{2,0,1:T(8,128)(2,1)} %bitcast.1) | data formatting | bytes 16777216 | tf_op jit(solution)/shard_map/all_to_all | solution.py:54
  219.8 4.7 fusion.221
  224.6 1.1 slice-done.1
  225.7 2.9 fusion.8
  228.6 3.5 all-to-all-start.1
  233.4 4.0 all-to-all-done.1
  237.4 0.7 broadcast_in_dim.30
  238.1 7.7 %all-to-all-start.2 = ((f32[16,10,256]{2,1,0:T(8,128)}), f32[16,10,256]{2,1,0:T(8,128)S(1)}, u32[]{:S(2)}, u32[]{:S(2)}) async-start(f32[16,10,256]{2,1,0:T(8,128)} %broadcast_in_dim.30), calls=%async_computation.2 | async-start | bytes 524288 | tf_op jit(solution)/shard_map/all_to_all | solution.py:16
  246.0 7.4 %all-to-all-done.2 = f32[16,10,256]{2,1,0:T(8,128)S(1)} async-done(((f32[16,10,256]{2,1,0:T(8,128)}), f32[16,10,256]{2,1,0:T(8,128)S(1)}, u32[]{:S(2)}, u32[]{:S(2)}) %all-to-all-start.2) | async-done | bytes 163872 | tf_op jit(solution)/shard_map/all_to_all | solution.py:16
  253.5 5.0 fusion.110
  259.2 5.9 %all-to-all-start.3 = ((f32[8,1,512]{2,1,0:T(1,128)}), f32[8,1,512]{2,1,0:T(1,128)S(1)}, u32[]{:S(2)}, u32[]{:S(2)}) async-start(f32[8,1,512]{2,1,0:T(1,128)} %broadcast_in_dim.31), calls=%async_computation.3 | async-start | bytes 32768 | tf_op jit(solution)/shard_map/all_to_all | solution.py:16
  265.1 10.0 %while.12 = (s32[]{:T(128)}, f32[512,512]{1,0:T(8,128)S(1)}, s32[4,2]{0,1:T(2,128)S(1)}, f32[4,128,128]{2,1,0:T(8,128)}, s32[]{:T(128)}) while((s32[]{:T(128)}, f32[512,512]{1,0:T(8,128)S(1)}, s32[4,2]{0,1:T(2,128)S(1)}, f32[4,128,128]{2,1,0:T(8,128)}, s32[]{:T(128)}) %tuple.53), condition=%wide.while_cond.1, body=%wide.while_body.1.sunk | while | flops 2 | bytes 132205 | solution.py:92
  265.7 1.9 bitcast_dynamic-update-slice_fusion.2
  268.2 1.9 bitcast_dynamic-update-slice_fusion.2
  270.7 1.9 bitcast_dynamic-update-slice_fusion.2
  273.2 1.9 bitcast_dynamic-update-slice_fusion.2
  275.1 40.1 %custom-call.41 = f32[4,128,128]{1,2,0:T(8,128)S(1)} custom-call(f32[4,128,128]{2,1,0:T(8,128)} %get-tuple-element.48), custom_call_target="InvertDiagBlocksLowerTriangular" | custom-call | tf_op jit(solution)/shard_map/jit(_solve_triangular)/triangular_solve | solution.py:92
  318.3 6.8 %fusion.112 = f32[1,10,256]{2,0,1:T(1,128)S(1)} fusion(f32[10,256,512]{2,1,0:T(8,128)} %param.12, f32[128,1]{0,1:T(1,128)S(1)} %convolution_bitcast_fusion.30, f32[128,1]{0,1:T(1,128)S(1)} %convolution_bitcast_fusion.28, f32[128,1]{0,1:T(1,128)S(1)} %convolution_bitcast_fusion.26, f32[128,1]{0,1:T(1,128)S(1)} %convolution_bitcast_fusion.25), kind=kOutput, calls=%fused_computation.191 | convolution fusion | flops 15730176 | bytes 5255168 | tf_op jit(solution)/shard_map/dot_general | solution.py:95
  325.1 13.6 %all_gather.13 = bf16[10,2048]{1,0:T(8,128)(2,1)S(1)} all-gather(bf16[10,256]{1,0:T(8,128)(2,1)S(1)} %fusion.208), channel_id=1, replica_groups=mesh['samp'=16,'feat'=8] {'feat'}, dimensions={1}, use_global_device_ids=true | all-gather | bytes 46080 | tf_op jit(solution)/shard_map/all_gather | solution.py:107
  338.7 4.7 fusion.222
  343.5 2.3 fusion.11
  345.8 8.8 %all_to_all.113 = f32[8,10,256]{2,1,0:T(8,128)S(1)} all-to-all(f32[8,10,256]{2,1,0:T(8,128)S(1)} %fusion.11), channel_id=1, replica_groups=mesh['samp'=16,'feat'=8] {'feat'}, dimensions={0} | all-to-all | bytes 163840 | tf_op jit(solution)/shard_map/all_to_all | solution.py:33
  354.7 10.2 %all_to_all.114 = f32[16,10,256]{2,1,0:T(8,128)S(1)} all-to-all(f32[16,10,256]{2,1,0:T(8,128)S(1)} %broadcast_in_dim.33), channel_id=1, replica_groups=mesh['samp'=16,'feat'=8] {'samp'}, dimensions={0} | all-to-all | bytes 327680 | tf_op jit(solution)/shard_map/all_to_all | solution.py:16
  365.5 0.6 broadcast_in_dim.32
  366.2 9.2 %all_to_all.115 = f32[8,1,1]{2,1,0:T(1,128)S(1)} all-to-all(f32[8,1,1]{2,1,0:T(1,128)S(1)} %broadcast_in_dim.32), channel_id=1, replica_groups=mesh['samp'=16,'feat'=8] {'feat'}, dimensions={0} | all-to-all | bytes 64 | tf_op jit(solution)/shard_map/all_to_all | solution.py:16
  375.4 1.2 broadcast_in_dim.34
  376.5 4.1 all-to-all-start.7
  381.2 3.9 all-to-all-done.7
  387.1 5.0 fusion.108
  392.1 7.7 %all_to_all.116 = f32[8,1,512]{2,1,0:T(1,128)S(1)} all-to-all(f32[8,1,512]{2,1,0:T(1,128)S(1)} %broadcast_in_dim.35), channel_id=1, replica_groups=mesh['samp'=16,'feat'=8] {'feat'}, dimensions={0} | all-to-all | bytes 32768 | tf_op jit(solution)/shard_map/all_to_all | solution.py:16
  402.8 6.8 %fusion.119 = f32[1,10,256]{2,0,1:T(1,128)S(1)} fusion(f32[10,256,512]{2,1,0:T(8,128)} %param.12, f32[128,1]{0,1:T(1,128)S(1)} %convolution_bitcast_fusion.18, f32[128,1]{0,1:T(1,128)S(1)} %convolution_bitcast_fusion.16, f32[128,1]{0,1:T(1,128)S(1)} %convolution_bitcast_fusion.14, f32[128,1]{0,1:T(1,128)S(1)} %convolution_bitcast_fusion.13), kind=kOutput, calls=%fused_computation.200 | convolution fusion | flops 15730176 | bytes 5255168 | tf_op jit(solution)/shard_map/dot_general | solution.py:95
  410.3 0.6 broadcast_in_dim.36
  410.9 7.7 %all_to_all.117 = f32[8,1,1]{2,1,0:T(1,128)S(1)} all-to-all(f32[8,1,1]{2,1,0:T(1,128)S(1)} %broadcast_in_dim.36), channel_id=1, replica_groups=mesh['samp'=16,'feat'=8] {'feat'}, dimensions={0} | all-to-all | bytes 64 | tf_op jit(solution)/shard_map/all_to_all | solution.py:16
  420.5 13.3 %all_gather.14 = bf16[10,2048]{1,0:T(8,128)(2,1)S(1)} all-gather(bf16[10,256]{1,0:T(8,128)(2,1)S(1)} %get-tuple-element.65), channel_id=1, replica_groups=mesh['samp'=16,'feat'=8] {'feat'}, dimensions={1}, use_global_device_ids=true | all-gather | bytes 46080 | tf_op jit(solution)/shard_map/all_gather | solution.py:107
  433.8 4.6 fusion.223
  438.4 5.6 fusion.14
  444.0 7.9 %all_to_all.118 = f32[8,10,256]{2,1,0:T(8,128)S(1)} all-to-all(f32[8,10,256]{2,1,0:T(8,128)S(1)} %fusion.14), channel_id=1, replica_groups=mesh['samp'=16,'feat'=8] {'feat'}, dimensions={0} | all-to-all | bytes 163840 | tf_op jit(solution)/shard_map/all_to_all | solution.py:33
  452.0 10.2 %all_to_all.119 = f32[16,10,256]{2,1,0:T(8,128)S(1)} all-to-all(f32[16,10,256]{2,1,0:T(8,128)S(1)} %broadcast_in_dim.37), channel_id=1, replica_groups=mesh['samp'=16,'feat'=8] {'samp'}, dimensions={0} | all-to-all | bytes 327680 | tf_op jit(solution)/shard_map/all_to_all | solution.py:16
  463.4 9.4 %all_to_all.120 = f32[8,1,1]{2,1,0:T(1,128)S(1)} all-to-all(f32[8,1,1]{2,1,0:T(1,128)S(1)} %broadcast_in_dim.38), channel_id=1, replica_groups=mesh['samp'=16,'feat'=8] {'feat'}, dimensions={0} | all-to-all | bytes 64 | tf_op jit(solution)/shard_map/all_to_all | solution.py:16
  474.7 5.0 fusion.106
  479.8 7.7 %all_to_all.121 = f32[8,1,512]{2,1,0:T(1,128)S(1)} all-to-all(f32[8,1,512]{2,1,0:T(1,128)S(1)} %broadcast_in_dim.39), channel_id=1, replica_groups=mesh['samp'=16,'feat'=8] {'feat'}, dimensions={0} | all-to-all | bytes 32768 | tf_op jit(solution)/shard_map/all_to_all | solution.py:16
  490.4 6.8 %fusion.126 = f32[1,10,256]{2,0,1:T(1,128)S(1)} fusion(f32[10,256,512]{2,1,0:T(8,128)} %param.12, f32[128,1]{0,1:T(1,128)S(1)} %convolution_bitcast_fusion.6, f32[128,1]{0,1:T(1,128)S(1)} %convolution_bitcast_fusion.4, f32[128,1]{0,1:T(1,128)S(1)} %convolution_bitcast_fusion.2, f32[128,1]{0,1:T(1,128)S(1)} %convolution_bitcast_fusion.1), kind=kOutput, calls=%fused_computation.209 | convolution fusion | flops 15730176 | bytes 5255168 | tf_op jit(solution)/shard_map/dot_general | solution.py:95
  498.4 7.7 %all_to_all.122 = f32[8,1,1]{2,1,0:T(1,128)S(1)} all-to-all(f32[8,1,1]{2,1,0:T(1,128)S(1)} %broadcast_in_dim.40), channel_id=1, replica_groups=mesh['samp'=16,'feat'=8] {'feat'}, dimensions={0} | all-to-all | bytes 64 | tf_op jit(solution)/shard_map/all_to_all | solution.py:16
  508.0 13.3 %all_gather.15 = bf16[10,2048]{1,0:T(8,128)(2,1)S(1)} all-gather(bf16[10,256]{1,0:T(8,128)(2,1)S(1)} %get-tuple-element.63), channel_id=1, replica_groups=mesh['samp'=16,'feat'=8] {'feat'}, dimensions={1}, use_global_device_ids=true | all-gather | bytes 46080 | tf_op jit(solution)/shard_map/all_gather | solution.py:107
  521.3 4.6 fusion.224
  525.9 5.6 fusion.17
  531.5 7.9 %all_to_all.123 = f32[8,10,256]{2,1,0:T(8,128)S(1)} all-to-all(f32[8,10,256]{2,1,0:T(8,128)S(1)} %fusion.17), channel_id=1, replica_groups=mesh['samp'=16,'feat'=8] {'feat'}, dimensions={0} | all-to-all | bytes 163840 | tf_op jit(solution)/shard_map/all_to_all | solution.py:33
  539.5 10.2 %all_to_all.124 = f32[16,10,256]{2,1,0:T(8,128)S(1)} all-to-all(f32[16,10,256]{2,1,0:T(8,128)S(1)} %broadcast_in_dim.41), channel_id=1, replica_groups=mesh['samp'=16,'feat'=8] {'samp'}, dimensions={0} | all-to-all | bytes 327680 | tf_op jit(solution)/shard_map/all_to_all | solution.py:16
  550.3 0.6 broadcast_in_dim.42
  551.0 9.2 %all_to_all.125 = f32[8,1,1]{2,1,0:T(1,128)S(1)} all-to-all(f32[8,1,1]{2,1,0:T(1,128)S(1)} %broadcast_in_dim.42), channel_id=1, replica_groups=mesh['samp'=16,'feat'=8] {'feat'}, dimensions={0} | all-to-all | bytes 64 | tf_op jit(solution)/shard_map/all_to_all | solution.py:16
  (135 shorter events, 24.2 us)
Async XLA Ops:
  6.5 201.7 %all-to-all-start = ((bf16[8,2048,256]{2,1,0:T(8,128)(2,1)}), bf16[8,2048,256]{2,1,0:T(8,128)(2,1)}, u32[]{:S(2)}, u32[]{:S(2)}) async-start(bf16[8,2048,256]{2,1,0:T(8,128)(2,1)} %bitcast.495), calls=%async_computation | async-start | bytes 16777216 | tf_op jit(solution)/shard_map/all_to_all | solution.py:54
  12.8 12.4 %copy-start = (f32[10,256]{1,0:T(8,128)S(1)}, f32[10,256]{1,0:T(8,128)}, u32[]{:S(2)}) copy-start(f32[10,256]{1,0:T(8,128)} %param.11) | copy-start | bytes 30724
  12.8 12.4 %copy-start.1 = (f32[512]{0:T(512)S(1)}, f32[512]{0:T(512)}, u32[]{:S(2)}) copy-start(f32[512]{0:T(512)} %param.13) | copy-start | bytes 6148
  12.8 110.2 %all-reduce.3.cloned.1.call-start = ((), (), s32[]{:S(2)}) async-start(), calls=%async_computation.18 | async-start | bytes 2097152 | tf_op jit(solution)/shard_map/psum | solution.py:82
  219.8 4.8 slice-start
  219.8 4.8 dynamic-slice-start
  219.8 5.9 %slice-start.1 = ((s8[8388608]{0:T(1024)(128)(4,1)}), s8[4194304]{0:T(1024)(128)(4,1)S(1)}, s32[]{:S(2)}) async-start(s8[8388608]{0:T(1024)(128)(4,1)} %bitcast.491), calls=%async_computation.20 | async-start | bytes 8388608
  228.6 8.7 %all-to-all-start.1 = ((f32[8,10,256]{2,1,0:T(8,128)}), f32[8,10,256]{2,1,0:T(8,128)S(1)}, u32[]{:S(2)}, u32[]{:S(2)}) async-start(f32[8,10,256]{2,1,0:T(8,128)} %fusion.8), calls=%async_computation.1 | async-start | bytes 262144 | tf_op jit(solution)/shard_map/all_to_all | solution.py:33
  238.1 15.3 %all-to-all-start.2 = ((f32[16,10,256]{2,1,0:T(8,128)}), f32[16,10,256]{2,1,0:T(8,128)S(1)}, u32[]{:S(2)}, u32[]{:S(2)}) async-start(f32[16,10,256]{2,1,0:T(8,128)} %broadcast_in_dim.30), calls=%async_computation.2 | async-start | bytes 524288 | tf_op jit(solution)/shard_map/all_to_all | solution.py:16
  259.2 56.1 %all-to-all-start.3 = ((f32[8,1,512]{2,1,0:T(1,128)}), f32[8,1,512]{2,1,0:T(1,128)S(1)}, u32[]{:S(2)}, u32[]{:S(2)}) async-start(f32[8,1,512]{2,1,0:T(1,128)} %broadcast_in_dim.31), calls=%async_computation.3 | async-start | bytes 32768 | tf_op jit(solution)/shard_map/all_to_all | solution.py:16
  325.1 18.4 %slice-start.2 = ((s8[8388608]{0:T(1024)(128)(4,1)}), s8[4194304]{0:T(1024)(128)(4,1)S(1)}, s32[]{:S(2)}) async-start(s8[8388608]{0:T(1024)(128)(4,1)} %bitcast.493), calls=%async_computation.21 | async-start | bytes 8388608
  338.7 4.8 slice-start.3
  376.5 8.6 %all-to-all-start.7 = ((f32[8,1,1]{2,1,0:T(1,128)}), f32[8,1,1]{2,1,0:T(1,128)S(1)}, u32[]{:S(2)}, u32[]{:S(2)}) async-start(f32[8,1,1]{2,1,0:T(1,128)} %broadcast_in_dim.34), calls=%async_computation.7 | async-start | bytes 8192 | tf_op jit(solution)/shard_map/all_to_all | solution.py:16
Sparse Core Ops, SparseCore 0:
  25.3 71.9 all-reduce.2
where the time goes:
time: 576 us; the launch traced here: 570 us
  blocking collectives  251 us (44%)
  other arithmetic  129 us (22%)
  matrix products  93.6 us (16%)
  local copies, waits for them, and re-layouts  30.1 us (5%)
  starting transfers between devices  27.6 us (5%)
  between operations  23.7 us (4%)
  waiting for transfers between devices  15.4 us (3%)
    all_gather x1, blocking collectives, on_device(): weights_b = lax.all_gather(weights_b, 'feat', axis=1, tiled=True)  96.5 us
    all_to_all x10, blocking collectives, copy_for_each(): lax.all_to_all(jnp.broadcast_to(shard[None], (devices, *shard.shape)), ax...  89.2 us
    another operation x14, other arithmetic, on_device(): factor = jnp.linalg.cholesky(gram_matrix)  78.8 us
    another operation x4, other arithmetic, precondition(): jax.scipy.linalg.solve_triangular(factor, weighted_coords, lower=True, tr...  40.3 us
    all_gather x3, blocking collectives, on_device(): gathered = lax.all_gather(gathered, 'feat', axis=1, tiled=True)  40.2 us
    all_to_all x3, blocking collectives, summed_on_arrival(): lax.all_to_all(in_blocks(shard, dim, devices), axis, 0, 0, tiled=True)  24.7 us
    dot_general x3, matrix products, precondition(): jnp.dot(basis_own, outer_coords, precision=lax.Precision.HIGHEST)  20.5 us
    dot_general x4, matrix products, class_logits(): lax.dot_general(rounded, row_features, contract_last, preferred_element_t...  18.7 us
  transfers between devices with their start and end apart: 6, of which 3 were waited for; matrix products, arithmetic and copies ran while one was open for 26% of the time, Pallas kernels for 0%

commit v1 on v0

--- a/solution.py
+++ b/solution.py
@@ -72,7 +72,8 @@
         return of_everyone(partial_cols, "samp")
 
     weights_b = weights.astype(jnp.bfloat16)
-    weights_b = lax.all_gather(weights_b, "feat", axis=1, tiled=True)
+    stack = jnp.stack([weights_b] * lax.axis_size("feat"))
+    weights_b = jnp.concatenate(lax.all_to_all(stack, "feat", 0, 0), axis=1)
     probabilities = column_softmax(class_logits(weights_b) / math.sqrt(F))
     gradient = feature_sums(probabilities - onehot) * (math.sqrt(F) / total_rows) + ridge * weights
     flat_local = sketch_basis.reshape(classes * local_cols, sketch_rank)

time: 576 us -> 577 us (level)
  blocking collectives: 251 us -> 154 us
  waiting for transfers between devices: 15.4 us -> 86.2 us
  starting transfers between devices: 27.6 us -> 52.5 us
    all_gather x1 -> x0, blocking collectives: 96.5 us -> none  [on_device(): weights_b = lax.all_gather(weights_b, 'feat', axis=1, tiled=True)]
    psum x1, waiting for transfers between devices: 0.01 us -> 70.8 us  [on_device(): gram_matrix = lax.psum(local_gram, 'feat')]
    all_to_all x0 -> x1, starting transfers between devices: none -> 23.9 us  [on_device(): weights_b = jnp.concatenate(lax.all_to_all(stack, 'feat', 0, 0), axis=1)]
  transfers between devices with their start and end apart: 6 -> 7, of which waited for: 3 -> 4; matrix products, arithmetic and copies ran while one was open for 26% -> 28% of each run, Pallas kernels for 0% -> 0%
where the time goes in v1:
time: 577 us; the launch traced here: 571 us
  blocking collectives  154 us (27%)
  other arithmetic  129 us (22%)
  matrix products  94.9 us (16%)
  waiting for transfers between devices  86.2 us (15%)
  starting transfers between devices  52.5 us (9%)
  local copies, waits for them, and re-layouts  30.1 us (5%)
  between operations  23.9 us (4%)
    all_to_all x10, blocking collectives, copy_for_each(): lax.all_to_all(jnp.broadcast_to(shard[None], (devices, *shard.shape)), ax...  89.3 us
    another operation x14, other arithmetic, on_device(): factor = jnp.linalg.cholesky(gram_matrix)  78.9 us
    psum x1, waiting for transfers between devices, on_device(): gram_matrix = lax.psum(local_gram, 'feat')  70.8 us
    another operation x4, other arithmetic, precondition(): jax.scipy.linalg.solve_triangular(factor, weighted_coords, lower=True, tr...  40.3 us
    all_gather x3, blocking collectives, on_device(): gathered = lax.all_gather(gathered, 'feat', axis=1, tiled=True)  40.2 us
    all_to_all x3, blocking collectives, summed_on_arrival(): lax.all_to_all(in_blocks(shard, dim, devices), axis, 0, 0, tiled=True)  24.7 us
    all_to_all x1, starting transfers between devices, on_device(): weights_b = jnp.concatenate(lax.all_to_all(stack, 'feat', 0, 0), axis=1)  23.9 us
    dot_general x3, matrix products, precondition(): jnp.dot(basis_own, outer_coords, precision=lax.Precision.HIGHEST)  20.5 us
  transfers between devices with their start and end apart: 7, of which 4 were waited for; matrix products, arithmetic and copies ran while one was open for 28% of the time, Pallas kernels for 0%

profile of v1, /device:TPU:1, one launch (start us, length us, event | category | flops | bytes accessed | tf_op | source)
XLA Modules:
  0.0 570.6 jit_solution(13249832406405929882)
XLA Ops:
  6.5 6.3 %all-to-all-start.1 = ((bf16[8,2048,256]{2,1,0:T(8,128)(2,1)}), bf16[8,2048,256]{2,1,0:T(8,128)(2,1)}, u32[]{:S(2)}, u32[]{:S(2)}) async-start(bf16[8,2048,256]{2,1,0:T(8,128)(2,1)} %bitcast.503), calls=%async_computation.1 | async-start | bytes 16777216 | tf_op jit(solution)/shard_map/all_to_all | solution.py:54
  12.9 12.5 %convolution_bitcast_fusion.1 = f32[512,512]{0,1:T(8,128)} fusion(f32[10,256,512]{2,1,0:T(8,128)} %param.12), kind=kOutput, calls=%fused_computation.15 | convolution fusion | flops 8053063680 | bytes 6291456 | tf_op jit(solution)/shard_map/dot_general | solution.py:80
  26.7 70.8 %all-reduce.3.cloned.1.call-done = f32[512,512]{0,1:T(8,128)} async-done(((f32[512,512]{0,1:T(8,128)}), f32[512,512]{0,1:T(8,128)}) %all-reduce.3.cloned.1.call-update) | async-done | bytes 1048592 | tf_op jit(solution)/shard_map/psum | solution.py:83
  97.5 1.6 copy.21
  99.1 1.4 fusion.57
  100.5 11.7 %cholesky.104 = f32[128,128]{1,0:T(8,128)S(1)} custom-call(f32[128,128]{1,0:T(8,128)S(1)} %cholesky.266), custom_call_target="Cholesky" | custom-call | tf_op jit(solution)/shard_map/jit(cholesky)/cholesky | solution.py:84
  112.4 9.8 %custom-call.33 = f32[1,128,128]{1,2,0:T(8,128)S(1)} custom-call(f32[1,128,128]{2,1,0:T(8,128)S(1)} %get-tuple-element.78), custom_call_target="InvertDiagBlocksLowerTriangular" | custom-call | tf_op jit(solution)/shard_map/jit(cholesky)/cholesky | solution.py:84
  122.9 11.7 %cholesky.217 = f32[128,128]{1,0:T(8,128)S(1)} custom-call(f32[128,128]{1,0:T(8,128)S(1)} %cholesky.270), custom_call_target="Cholesky" | custom-call | tf_op jit(solution)/shard_map/jit(cholesky)/cholesky | solution.py:84
  134.7 10.3 %custom-call.34 = f32[1,128,128]{1,2,0:T(8,128)S(1)} custom-call(f32[1,128,128]{2,1,0:T(8,128)S(1)} %get-tuple-element.75), custom_call_target="InvertDiagBlocksLowerTriangular" | custom-call | tf_op jit(solution)/shard_map/jit(cholesky)/cholesky | solution.py:84
  145.6 11.7 %cholesky.238 = f32[128,128]{1,0:T(8,128)S(1)} custom-call(f32[128,128]{1,0:T(8,128)S(1)} %cholesky.275), custom_call_target="Cholesky" | custom-call | tf_op jit(solution)/shard_map/jit(cholesky)/cholesky | solution.py:84
  157.3 9.8 %custom-call.35 = f32[1,128,128]{1,2,0:T(8,128)S(1)} custom-call(f32[1,128,128]{2,1,0:T(8,128)S(1)} %get-tuple-element.72), custom_call_target="InvertDiagBlocksLowerTriangular" | custom-call | tf_op jit(solution)/shard_map/jit(cholesky)/cholesky | solution.py:84
  167.8 11.7 %cholesky.255 = f32[128,128]{1,0:T(8,128)S(1)} custom-call(f32[128,128]{1,0:T(8,128)S(1)} %convolution_subtract_fusion.2), custom_call_target="Cholesky" | custom-call | tf_op jit(solution)/shard_map/jit(cholesky)/cholesky | solution.py:84
  179.5 0.7 compare_reduce_fusion.2
  180.9 23.9 %all-to-all-start = ((bf16[8,10,256]{2,1,0:T(8,128)(2,1)}), bf16[8,10,256]{2,1,0:T(8,128)(2,1)S(1)}, u32[]{:S(2)}, u32[]{:S(2)}) async-start(bf16[8,10,256]{2,1,0:T(8,128)(2,1)} %stack.2), calls=%async_computation | async-start | bytes 131072 | tf_op jit(solution)/shard_map/all_to_all | solution.py:76
  204.8 0.7 compare_reduce_fusion.1
  207.3 11.6 %copy.17 = bf16[2048,8,256]{0,2,1:T(8,128)(2,1)} copy(bf16[2048,8,256]{2,0,1:T(8,128)(2,1)} %bitcast.2) | data formatting | bytes 16777216 | tf_op jit(solution)/shard_map/all_to_all | solution.py:54
  218.9 5.8 %fusion.224 = (f32[2048]{0:T(1024)S(1)}, f32[10,2048]{1,0:T(8,128)S(1)}) fusion(bf16[8,2048,256]{2,1,0:T(8,128)(2,1)} %all-to-all-done.1, bf16[8,10,256]{2,1,0:T(8,128)(2,1)S(1)} %all-to-all-done), kind=kOutput, calls=%fused_computation.311 | convolution fusion | flops 83924992 | bytes 8519680 | tf_op jit(solution)/shard_map/dot_general | solution.py:63
  224.8 2.9 fusion.9
  227.8 4.8 all-to-all-start.2
  233.9 4.0 all-to-all-done.2
  237.8 0.7 broadcast_in_dim.30
  238.6 7.6 %all-to-all-start.3 = ((f32[16,10,256]{2,1,0:T(8,128)}), f32[16,10,256]{2,1,0:T(8,128)S(1)}, u32[]{:S(2)}, u32[]{:S(2)}) async-start(f32[16,10,256]{2,1,0:T(8,128)} %broadcast_in_dim.30), calls=%async_computation.3 | async-start | bytes 524288 | tf_op jit(solution)/shard_map/all_to_all | solution.py:16
  246.3 7.4 %all-to-all-done.3 = f32[16,10,256]{2,1,0:T(8,128)S(1)} async-done(((f32[16,10,256]{2,1,0:T(8,128)}), f32[16,10,256]{2,1,0:T(8,128)S(1)}, u32[]{:S(2)}, u32[]{:S(2)}) %all-to-all-start.3) | async-done | bytes 163872 | tf_op jit(solution)/shard_map/all_to_all | solution.py:16
  253.8 5.0 fusion.112
  259.4 5.7 all-to-all-start.4
  265.2 10.5 %while.12 = (s32[]{:T(128)}, f32[512,512]{1,0:T(8,128)S(1)}, s32[4,2]{0,1:T(2,128)S(1)}, f32[4,128,128]{2,1,0:T(8,128)}, s32[]{:T(128)}) while((s32[]{:T(128)}, f32[512,512]{1,0:T(8,128)S(1)}, s32[4,2]{0,1:T(2,128)S(1)}, f32[4,128,128]{2,1,0:T(8,128)}, s32[]{:T(128)}) %tuple.53), condition=%wide.while_cond.1, body=%wide.while_body.1.sunk | while | flops 2 | bytes 132205 | solution.py:93
  265.8 2.0 bitcast_dynamic-update-slice_fusion.2
  268.4 2.0 bitcast_dynamic-update-slice_fusion.2
  271.1 2.0 bitcast_dynamic-update-slice_fusion.2
  273.7 2.0 bitcast_dynamic-update-slice_fusion.2
  275.6 40.1 %custom-call.41 = f32[4,128,128]{1,2,0:T(8,128)S(1)} custom-call(f32[4,128,128]{2,1,0:T(8,128)} %get-tuple-element.48), custom_call_target="InvertDiagBlocksLowerTriangular" | custom-call | tf_op jit(solution)/shard_map/jit(_solve_triangular)/triangular_solve | solution.py:93
  318.8 6.8 %fusion.114 = f32[1,10,256]{2,0,1:T(1,128)S(1)} fusion(f32[10,256,512]{2,1,0:T(8,128)} %param.12, f32[128,1]{0,1:T(1,128)S(1)} %convolution_bitcast_fusion.31, f32[128,1]{0,1:T(1,128)S(1)} %convolution_bitcast_fusion.29, f32[128,1]{0,1:T(1,128)S(1)} %convolution_bitcast_fusion.27, f32[128,1]{0,1:T(1,128)S(1)} %convolution_bitcast_fusion.26), kind=kOutput, calls=%fused_computation.193 | convolution fusion | flops 15730176 | bytes 5255168 | tf_op jit(solution)/shard_map/dot_general | solution.py:96
  325.6 13.6 %all_gather.9 = bf16[10,2048]{1,0:T(8,128)(2,1)S(1)} all-gather(bf16[10,256]{1,0:T(8,128)(2,1)S(1)} %fusion.211), channel_id=1, replica_groups=mesh['samp'=16,'feat'=8] {'feat'}, dimensions={1}, use_global_device_ids=true | all-gather | bytes 46080 | tf_op jit(solution)/shard_map/all_gather | solution.py:108
  339.2 4.7 fusion.225
  344.0 2.3 fusion.12
  346.3 8.8 %all_to_all.118 = f32[8,10,256]{2,1,0:T(8,128)S(1)} all-to-all(f32[8,10,256]{2,1,0:T(8,128)S(1)} %fusion.12), channel_id=1, replica_groups=mesh['samp'=16,'feat'=8] {'feat'}, dimensions={0} | all-to-all | bytes 163840 | tf_op jit(solution)/shard_map/all_to_all | solution.py:33
  355.2 10.2 %all_to_all.119 = f32[16,10,256]{2,1,0:T(8,128)S(1)} all-to-all(f32[16,10,256]{2,1,0:T(8,128)S(1)} %broadcast_in_dim.33), channel_id=1, replica_groups=mesh['samp'=16,'feat'=8] {'samp'}, dimensions={0} | all-to-all | bytes 327680 | tf_op jit(solution)/shard_map/all_to_all | solution.py:16
  366.0 0.6 broadcast_in_dim.32
  366.7 9.2 %all_to_all.120 = f32[8,1,1]{2,1,0:T(1,128)S(1)} all-to-all(f32[8,1,1]{2,1,0:T(1,128)S(1)} %broadcast_in_dim.32), channel_id=1, replica_groups=mesh['samp'=16,'feat'=8] {'feat'}, dimensions={0} | all-to-all | bytes 64 | tf_op jit(solution)/shard_map/all_to_all | solution.py:16
  375.9 1.2 broadcast_in_dim.34
  377.0 4.1 all-to-all-start.8
  381.8 3.9 all-to-all-done.8
  387.6 5.0 fusion.110
  392.7 7.7 %all_to_all.121 = f32[8,1,512]{2,1,0:T(1,128)S(1)} all-to-all(f32[8,1,512]{2,1,0:T(1,128)S(1)} %broadcast_in_dim.35), channel_id=1, replica_groups=mesh['samp'=16,'feat'=8] {'feat'}, dimensions={0} | all-to-all | bytes 32768 | tf_op jit(solution)/shard_map/all_to_all | solution.py:16
  403.4 6.8 %fusion.121 = f32[1,10,256]{2,0,1:T(1,128)S(1)} fusion(f32[10,256,512]{2,1,0:T(8,128)} %param.12, f32[128,1]{0,1:T(1,128)S(1)} %convolution_bitcast_fusion.19, f32[128,1]{0,1:T(1,128)S(1)} %convolution_bitcast_fusion.17, f32[128,1]{0,1:T(1,128)S(1)} %convolution_bitcast_fusion.15, f32[128,1]{0,1:T(1,128)S(1)} %convolution_bitcast_fusion.14), kind=kOutput, calls=%fused_computation.202 | convolution fusion | flops 15730176 | bytes 5255168 | tf_op jit(solution)/shard_map/dot_general | solution.py:96
  410.8 0.6 broadcast_in_dim.36
  411.5 7.7 %all_to_all.122 = f32[8,1,1]{2,1,0:T(1,128)S(1)} all-to-all(f32[8,1,1]{2,1,0:T(1,128)S(1)} %broadcast_in_dim.36), channel_id=1, replica_groups=mesh['samp'=16,'feat'=8] {'feat'}, dimensions={0} | all-to-all | bytes 64 | tf_op jit(solution)/shard_map/all_to_all | solution.py:16
  421.0 13.3 %all_gather.10 = bf16[10,2048]{1,0:T(8,128)(2,1)S(1)} all-gather(bf16[10,256]{1,0:T(8,128)(2,1)S(1)} %get-tuple-element.65), channel_id=1, replica_groups=mesh['samp'=16,'feat'=8] {'feat'}, dimensions={1}, use_global_device_ids=true | all-gather | bytes 46080 | tf_op jit(solution)/shard_map/all_gather | solution.py:108
  434.3 4.6 fusion.226
  438.9 5.6 fusion.15
  444.6 7.9 %all_to_all.123 = f32[8,10,256]{2,1,0:T(8,128)S(1)} all-to-all(f32[8,10,256]{2,1,0:T(8,128)S(1)} %fusion.15), channel_id=1, replica_groups=mesh['samp'=16,'feat'=8] {'feat'}, dimensions={0} | all-to-all | bytes 163840 | tf_op jit(solution)/shard_map/all_to_all | solution.py:33
  452.6 10.2 %all_to_all.124 = f32[16,10,256]{2,1,0:T(8,128)S(1)} all-to-all(f32[16,10,256]{2,1,0:T(8,128)S(1)} %broadcast_in_dim.37), channel_id=1, replica_groups=mesh['samp'=16,'feat'=8] {'samp'}, dimensions={0} | all-to-all | bytes 327680 | tf_op jit(solution)/shard_map/all_to_all | solution.py:16
  463.9 9.5 %all_to_all.125 = f32[8,1,1]{2,1,0:T(1,128)S(1)} all-to-all(f32[8,1,1]{2,1,0:T(1,128)S(1)} %broadcast_in_dim.38), channel_id=1, replica_groups=mesh['samp'=16,'feat'=8] {'feat'}, dimensions={0} | all-to-all | bytes 64 | tf_op jit(solution)/shard_map/all_to_all | solution.py:16
  475.3 5.0 fusion.108
  480.3 7.7 %all_to_all.126 = f32[8,1,512]{2,1,0:T(1,128)S(1)} all-to-all(f32[8,1,512]{2,1,0:T(1,128)S(1)} %broadcast_in_dim.39), channel_id=1, replica_groups=mesh['samp'=16,'feat'=8] {'feat'}, dimensions={0} | all-to-all | bytes 32768 | tf_op jit(solution)/shard_map/all_to_all | solution.py:16
  491.0 6.8 %fusion.128 = f32[1,10,256]{2,0,1:T(1,128)S(1)} fusion(f32[10,256,512]{2,1,0:T(8,128)} %param.12, f32[128,1]{0,1:T(1,128)S(1)} %convolution_bitcast_fusion.7, f32[128,1]{0,1:T(1,128)S(1)} %convolution_bitcast_fusion.5, f32[128,1]{0,1:T(1,128)S(1)} %convolution_bitcast_fusion.3, f32[128,1]{0,1:T(1,128)S(1)} %convolution_bitcast_fusion.2), kind=kOutput, calls=%fused_computation.211 | convolution fusion | flops 15730176 | bytes 5255168 | tf_op jit(solution)/shard_map/dot_general | solution.py:96
  499.0 7.7 %all_to_all.127 = f32[8,1,1]{2,1,0:T(1,128)S(1)} all-to-all(f32[8,1,1]{2,1,0:T(1,128)S(1)} %broadcast_in_dim.40), channel_id=1, replica_groups=mesh['samp'=16,'feat'=8] {'feat'}, dimensions={0} | all-to-all | bytes 64 | tf_op jit(solution)/shard_map/all_to_all | solution.py:16
  508.6 13.3 %all_gather.11 = bf16[10,2048]{1,0:T(8,128)(2,1)S(1)} all-gather(bf16[10,256]{1,0:T(8,128)(2,1)S(1)} %get-tuple-element.63), channel_id=1, replica_groups=mesh['samp'=16,'feat'=8] {'feat'}, dimensions={1}, use_global_device_ids=true | all-gather | bytes 46080 | tf_op jit(solution)/shard_map/all_gather | solution.py:108
  521.9 4.6 fusion.227
  526.5 5.6 fusion.18
  532.1 7.9 %all_to_all.128 = f32[8,10,256]{2,1,0:T(8,128)S(1)} all-to-all(f32[8,10,256]{2,1,0:T(8,128)S(1)} %fusion.18), channel_id=1, replica_groups=mesh['samp'=16,'feat'=8] {'feat'}, dimensions={0} | all-to-all | bytes 163840 | tf_op jit(solution)/shard_map/all_to_all | solution.py:33
  540.1 10.2 %all_to_all.129 = f32[16,10,256]{2,1,0:T(8,128)S(1)} all-to-all(f32[16,10,256]{2,1,0:T(8,128)S(1)} %broadcast_in_dim.41), channel_id=1, replica_groups=mesh['samp'=16,'feat'=8] {'samp'}, dimensions={0} | all-to-all | bytes 327680 | tf_op jit(solution)/shard_map/all_to_all | solution.py:16
  550.9 0.6 broadcast_in_dim.42
  551.6 9.2 %all_to_all.130 = f32[8,1,1]{2,1,0:T(1,128)S(1)} all-to-all(f32[8,1,1]{2,1,0:T(1,128)S(1)} %broadcast_in_dim.42), channel_id=1, replica_groups=mesh['samp'=16,'feat'=8] {'feat'}, dimensions={0} | all-to-all | bytes 64 | tf_op jit(solution)/shard_map/all_to_all | solution.py:16
  (134 shorter events, 25.0 us)
Async XLA Ops:
  6.5 173.7 %all-to-all-start.1 = ((bf16[8,2048,256]{2,1,0:T(8,128)(2,1)}), bf16[8,2048,256]{2,1,0:T(8,128)(2,1)}, u32[]{:S(2)}, u32[]{:S(2)}) async-start(bf16[8,2048,256]{2,1,0:T(8,128)(2,1)} %bitcast.503), calls=%async_computation.1 | async-start | bytes 16777216 | tf_op jit(solution)/shard_map/all_to_all | solution.py:54
  12.8 12.6 %copy-start.1 = (f32[10,256]{1,0:T(8,128)S(1)}, f32[10,256]{1,0:T(8,128)}, u32[]{:S(2)}) copy-start(f32[10,256]{1,0:T(8,128)} %param.11) | copy-start | bytes 30724
  12.8 12.6 %copy-start.2 = (f32[512]{0:T(512)S(1)}, f32[512]{0:T(512)}, u32[]{:S(2)}) copy-start(f32[512]{0:T(512)} %param.13) | copy-start | bytes 6148
  12.8 84.7 %all-reduce.3.cloned.1.call-start = ((), (), s32[]{:S(2)}) async-start(), calls=%async_computation.19 | async-start | bytes 2097152 | tf_op jit(solution)/shard_map/psum | solution.py:83
  180.9 38.1 %all-to-all-start = ((bf16[8,10,256]{2,1,0:T(8,128)(2,1)}), bf16[8,10,256]{2,1,0:T(8,128)(2,1)S(1)}, u32[]{:S(2)}, u32[]{:S(2)}) async-start(bf16[8,10,256]{2,1,0:T(8,128)(2,1)} %stack.2), calls=%async_computation | async-start | bytes 131072 | tf_op jit(solution)/shard_map/all_to_all | solution.py:76
  218.9 5.9 %dynamic-slice-start = ((s32[16384]{0:T(1024)}, s32[]{:T(128)}), s32[2048]{0:T(1024)S(1)}, s32[]{:S(2)}) async-start(s32[16384]{0:T(1024)} %param.10, s32[]{:T(128)} %select_n.7), calls=%async_computation.22 | async-start | bytes 16896 | tf_op jit(solution)/shard_map/dynamic_slice | solution.py:57
  218.9 5.9 %copy-start = (bf16[2048,8,256]{0,2,1:T(8,128)(2,1)S(1)}, bf16[2048,8,256]{0,2,1:T(8,128)(2,1)}, u32[]{:S(2)}) copy-start(bf16[2048,8,256]{0,2,1:T(8,128)(2,1)} %copy.17) | copy-start | bytes 25165828
  227.8 10.1 %all-to-all-start.2 = ((f32[8,10,256]{2,1,0:T(8,128)}), f32[8,10,256]{2,1,0:T(8,128)S(1)}, u32[]{:S(2)}, u32[]{:S(2)}) async-start(f32[8,10,256]{2,1,0:T(8,128)} %fusion.9), calls=%async_computation.2 | async-start | bytes 262144 | tf_op jit(solution)/shard_map/all_to_all | solution.py:33
  238.6 15.2 %all-to-all-start.3 = ((f32[16,10,256]{2,1,0:T(8,128)}), f32[16,10,256]{2,1,0:T(8,128)S(1)}, u32[]{:S(2)}, u32[]{:S(2)}) async-start(f32[16,10,256]{2,1,0:T(8,128)} %broadcast_in_dim.30), calls=%async_computation.3 | async-start | bytes 524288 | tf_op jit(solution)/shard_map/all_to_all | solution.py:16
  259.4 56.3 %all-to-all-start.4 = ((f32[8,1,512]{2,1,0:T(1,128)}), f32[8,1,512]{2,1,0:T(1,128)S(1)}, u32[]{:S(2)}, u32[]{:S(2)}) async-start(f32[8,1,512]{2,1,0:T(1,128)} %broadcast_in_dim.31), calls=%async_computation.4 | async-start | bytes 32768 | tf_op jit(solution)/shard_map/all_to_all | solution.py:16
  325.6 18.4 %slice-start = ((s8[8388608]{0:T(1024)(128)(4,1)}), s8[4194304]{0:T(1024)(128)(4,1)S(1)}, s32[]{:S(2)}) async-start(s8[8388608]{0:T(1024)(128)(4,1)} %bitcast.501), calls=%async_computation.20 | async-start | bytes 8388608
  339.2 4.8 slice-start.1
  377.0 8.7 %all-to-all-start.8 = ((f32[8,1,1]{2,1,0:T(1,128)}), f32[8,1,1]{2,1,0:T(1,128)S(1)}, u32[]{:S(2)}, u32[]{:S(2)}) async-start(f32[8,1,1]{2,1,0:T(1,128)} %broadcast_in_dim.34), calls=%async_computation.8 | async-start | bytes 8192 | tf_op jit(solution)/shard_map/all_to_all | solution.py:16
Sparse Core Ops, SparseCore 0:
  25.5 71.9 all-reduce.2
